TPU v7x, 256 devices: a whole 4x4x8 slice. The times are simulated.
256 devices in a mesh: row: 32 (over y, x, core), col: 8 (over z).
Axes of the slice: x: 4, y: 4, z: 8, core: 2. Of those that a mesh axis runs over, the one named last changes fastest.
Arguments:
- integrals: bfloat16 [1280, 32, 8192], P('row', None, 'col'), may hold values from -6 to 6
- coeffs: bfloat16 [40960, 4096], P('row', 'col'), may hold values from -0.0546875 to 0.0546875
- mask: int32 [1280, 8], replicated, may hold values from 0 to 1, as said below
- offsets: int32 [1281], replicated, may hold values from 0 to 30720, as said below
- atom_of_slot: int32 [1280], replicated, may hold values from 0 to 1279, as said below
Outputs:
- half_transformed: bfloat16 [4096, 8192], P('row', 'col')
Inputs may be any that keep to these rules, and one draw needn't show every extreme that they name: `mask`: 1 marks a significant pair of an atom and a block of 64 window functions. offsets[0] = 0 and offsets[a + 1] - offsets[a] is atom a's number of basis functions, 16 to 32; atoms 2k and 2k + 1 together have 3 * 16; rows of an atom's padded block past its number are padding. `atom_of_slot`: a permutation of the atoms; slot k is held by atom owner k // 40 along row, and atom a's AO-row owner is a // 40; one atom owner holds at least one and at most 2 atoms of any one AO-row owner, and exactly 2 for some pairs.
All inputs are finite; a program needn't handle non-finite values.
Results may differ from a plain program's by a relative error of at most 0.015.
Values may be sent and summed in bfloat16 or wider, within the bound.
A program may use at most 256 MiB of HBM per device.

v0:
```python
import jax
import jax.numpy as jnp
from jax import lax
from jax.sharding import PartitionSpec as P


def body(integrals, coeffs, mask, offsets, atom_of_slot):
    n_row = lax.axis_size("row")
    own_row = lax.axis_index("row")
    own_col = lax.axis_index("col")
    per_dev, atom_w, row_width = integrals.shape
    slots_cap = max(2, -(-per_dev // n_row))
    counter = jnp.arange(per_dev, dtype=jnp.int32)
    slot_count = n_row * slots_cap
    mine_slots = lax.dynamic_slice_in_dim(atom_of_slot, own_row * per_dev, per_dev)
    target = mine_slots // per_dev
    before = (target[None, :] == target[:, None]) & (counter[None, :] < counter[:, None])
    arrival_rank = jnp.sum(before.astype(jnp.int32), axis=1)
    position = target * slots_cap + arrival_rank
    placing = (jnp.arange(slot_count, dtype=jnp.int32)[:, None] == position[None, :]).astype(
        jnp.bfloat16
    )
    outgoing = jnp.dot(
        placing, integrals.reshape(per_dev, atom_w * row_width), preferred_element_type=jnp.bfloat16
    )
    outgoing = outgoing.reshape(n_row, slots_cap, atom_w * row_width)
    incoming = lax.all_to_all(outgoing, "row", split_axis=0, concat_axis=0, tiled=True)
    holders = atom_of_slot.reshape(n_row, per_dev)
    is_mine = holders // per_dev == own_row
    arrival = jnp.cumsum(is_mine.astype(jnp.int32), axis=1) - 1
    slot_of = jnp.arange(n_row, dtype=jnp.int32)[:, None] * slots_cap + arrival
    local_atom = holders - own_row * per_dev
    pick_atom = (
        (local_atom.reshape(-1)[:, None] == counter[None, :]) & is_mine.reshape(-1)[:, None]
    ).astype(jnp.float32)
    pick_slot = (
        slot_of.reshape(-1)[:, None] == jnp.arange(slot_count, dtype=jnp.int32)[None, :]
    ).astype(jnp.float32)
    gather_matrix = jnp.dot(pick_atom.T, pick_slot).astype(jnp.bfloat16)
    ordered = jnp.dot(
        gather_matrix,
        incoming.reshape(slot_count, atom_w * row_width),
        preferred_element_type=jnp.bfloat16,
    )
    ordered = ordered.reshape(per_dev, atom_w, row_width)
    bounds = lax.dynamic_slice_in_dim(offsets, own_row * per_dev, per_dev + 1)
    lengths = bounds[1:] - bounds[:-1]
    significant = lax.dynamic_slice(mask, (own_row * per_dev, own_col), (per_dev, 1))[:, 0] > 0
    keep_rows = (jnp.arange(atom_w, dtype=jnp.int32)[None, :] < lengths[:, None]) & significant[
        :, None
    ]
    blocks = ordered * keep_rows[:, :, None].astype(jnp.bfloat16)
    bucket_edges = [0, per_dev]
    kept_rows = blocks.reshape(per_dev * atom_w, row_width)
    coeff_piece = lax.all_gather(coeffs, "col", axis=1, tiled=True)
    low_row = bucket_edges[0] * atom_w
    high_row = bucket_edges[1] * atom_w

    def product(low_row=low_row, high_row=high_row):
        return lax.dot_general(
            coeff_piece, kept_rows, (((0,), (0,)), ((), ())), preferred_element_type=jnp.float32
        )

    bucket_term = product()
    partial_sums = bucket_term.astype(jnp.bfloat16)
    result = lax.psum_scatter(partial_sums, "row", scatter_dimension=0, tiled=True).astype(
        jnp.float32
    )
    return result.astype(jnp.bfloat16)


def solution(mesh):
    in_specs = (P("row", None, "col"), P("row", "col"), P(), P(), P())
    out_specs = P("row", "col")
    return jax.shard_map(body, mesh=mesh, in_specs=in_specs, out_specs=out_specs, check_vma=False)
```

profile of v0, /device:TPU:2, one launch (start us, length us, event | category | flops | bytes accessed | tf_op | source)
XLA Modules:
  0.0 260.2 jit_solution(1185108357489608472)
XLA Ops:
  6.5 0.7 all-gather.2.cloned.1.call-update
  7.3 5.3 %reshape.121 = bf16[40,32768,1]{1,0,2:T(8,128)(2,1)} reshape(bf16[40,32,1024]{2,1,0:T(8,128)(2,1)} %param.5) | data formatting | bytes 5242880 | tf_op jit(solution)/shard_map/reshape | solution.py:24
  12.6 0.1 and_select_fusion
  12.6 0.2 convert_reduce_fusion
  12.8 0.1 multiply_add_fusion.1
  12.9 3.0 %fusion.17 = bf16[32,2,32768]{2,0,1:T(8,128)(2,1)S(1)} fusion(bf16[40,32768,1]{1,0,2:T(8,128)(2,1)} %reshape.121, s32[40]{0:T(128)S(1)} %multiply_add_fusion.1, s32[32,2]{0,1:T(2,128)S(1)} %multiply_add_fusion), kind=kOutput, calls=%fused_computation.13 | convolution fusion | flops 167774720 | bytes 6816160 | tf_op jit(solution)/shard_map/dot_general | solution.py:23
  16.0 6.3 %copy.15 = bf16[32,2,32768]{2,1,0:T(2,128)(2,1)} copy(bf16[32,2,32768]{2,0,1:T(8,128)(2,1)S(1)} %fusion.17) | data formatting | bytes 8388608 | tf_op jit(solution)/shard_map/dot_general | solution.py:23
  22.2 7.7 %all-to-all-start = ((bf16[32,2,32768]{2,1,0:T(2,128)(2,1)}), bf16[32,2,32768]{2,1,0:T(2,128)(2,1)}, u32[]{:S(2)}, u32[]{:S(2)}) async-start(bf16[32,2,32768]{2,1,0:T(2,128)(2,1)} %copy.15), calls=%async_computation | async-start | bytes 8388608 | tf_op jit(solution)/shard_map/all_to_all | solution.py:27
  29.9 0.2 reduce-scatter.4.cloned.1.call-start
  30.2 0.1 and.41
  30.3 0.1 div.18
  30.4 0.2 reduce_window_sum.11
  30.6 0.1 add_add_fusion
  30.7 0.1 add.46
  30.7 0.8 dynamic_slice.10
  31.5 0.8 compare_bitcast_fusion
  32.4 49.0 %all-to-all-done = bf16[32,2,32768]{2,1,0:T(2,128)(2,1)} async-done(((bf16[32,2,32768]{2,1,0:T(2,128)(2,1)}), bf16[32,2,32768]{2,1,0:T(2,128)(2,1)}, u32[]{:S(2)}, u32[]{:S(2)}) %all-to-all-start) | async-done | bytes 4194336 | tf_op jit(solution)/shard_map/all_to_all | solution.py:27
  81.3 7.2 %reshape.119 = bf16[64,32768]{1,0:T(8,128)(2,1)} reshape(bf16[32,2,32768]{2,1,0:T(2,128)(2,1)} %all-to-all-done) | data formatting | bytes 8388608 | tf_op jit(solution)/shard_map/reshape | solution.py:42
  88.6 3.9 %fusion.3 = bf16[40,32,1024]{2,0,1:T(8,128)(2,1)S(1)} fusion(bf16[8,32,8,1024]{3,2,1,0:T(8,128)(2,1)} %bitcast.20, bf16[40,32]{0,1:T(8,128)(2,1)S(1)} %fusion.24, s32[1280]{0:T(1024)S(1)} %add.46, s32[1280]{0:T(1024)S(1)} %get-tuple-element.7, pred[1280]{0:T(1024)(128)(4,1)S(1)} %get-tuple-element.5), kind=kOutput, calls=%fused_computation.4 | convolution fusion | flops 179755520 | bytes 6829824 | tf_op jit(solution)/shard_map/dot_general | solution.py:40
  92.5 2.9 %copy.17 = bf16[40,32,1024]{2,1,0:T(8,128)(2,1)} copy(bf16[40,32,1024]{2,0,1:T(8,128)(2,1)S(1)} %fusion.3) | data formatting | bytes 5242880 | tf_op jit(solution)/shard_map/mul | solution.py:52
  95.4 30.4 %all-gather.2.cloned.1.call-done = bf16[1280,4096]{1,0:T(8,128)(2,1)} async-done(((bf16[1280,512]{1,0:T(8,128)(2,1)}), bf16[1280,4096]{1,0:T(8,128)(2,1)}) %all-gather.2.cloned.1.call-update) | async-done | bytes 10485776 | tf_op jit(solution)/shard_map/all_gather | solution.py:55
  125.8 16.8 %convert_bitcast_fusion = bf16[4096,1024]{0,1:T(8,128)(2,1)} fusion(bf16[1280,1024]{1,0:T(8,128)(2,1)} %bitcast.21, bf16[1280,4096]{1,0:T(8,128)(2,1)} %all-gather.2.cloned.1.call-done), kind=kOutput, calls=%fused_computation | convolution fusion | flops 10741612544 | bytes 21495808 | tf_op jit(solution)/shard_map/dot_general | solution.py:60
  142.6 12.0 %copy.19 = bf16[4096,1024]{1,0:T(8,128)(2,1)} copy(bf16[4096,1024]{0,1:T(8,128)(2,1)} %convert_bitcast_fusion) | data formatting | bytes 16777216
  154.6 98.8 %reduce-scatter.4.cloned.1.call-done = bf16[128,1024]{1,0:T(8,128)(2,1)} async-done(((bf16[4096,1024]{1,0:T(8,128)(2,1)}), bf16[128,1024]{1,0:T(8,128)(2,1)}) %reduce-scatter.4.cloned.1.call-update) | async-done | bytes 262160 | tf_op jit(solution)/shard_map/reduce_scatter | solution.py:66
  (11 shorter events, 0.1 us)
Async XLA Ops:
  6.5 6.0 %copy-start = (s32[1280]{0:T(1024)S(1)}, s32[1280]{0:T(1024)}, u32[]{:S(2)}) copy-start(s32[1280]{0:T(1024)} %param.9) | copy-start | bytes 15364
  6.5 119.3 %all-gather.2.cloned.1.call-start = ((), (), s32[]{:S(2)}) async-start(), calls=%async_computation.2 | async-start | bytes 11796480 | tf_op jit(solution)/shard_map/all_gather | solution.py:55
  22.2 59.1 %all-to-all-start = ((bf16[32,2,32768]{2,1,0:T(2,128)(2,1)}), bf16[32,2,32768]{2,1,0:T(2,128)(2,1)}, u32[]{:S(2)}, u32[]{:S(2)}) async-start(bf16[32,2,32768]{2,1,0:T(2,128)(2,1)} %copy.15), calls=%async_computation | async-start | bytes 8388608 | tf_op jit(solution)/shard_map/all_to_all | solution.py:27
  29.9 223.5 %reduce-scatter.4.cloned.1.call-start = ((), (), s32[]{:S(2)}) async-start(), calls=%async_computation.3 | async-start | bytes 8650752 | tf_op jit(solution)/shard_map/reduce_scatter | solution.py:66
Sparse Core Ops, SparseCore 0:
  9.1 116.6 all-gather.1
  154.7 98.6 reduce-scatter.3
where the time goes:
time: 261 us; the launch traced here: 260 us
  waiting for transfers between devices  179 us (69%)
  local copies, waits for them, and re-layouts  34.7 us (13%)
  matrix products  23.7 us (9%)
  between operations  13.5 us (5%)
  starting transfers between devices  7.9 us (3%)
    reduce_scatter x1, waiting for transfers between devices, body(): lax.psum_scatter(partial_sums, 'row', scatter_dimension=0, tiled=True)  98.8 us
    all_to_all x1, waiting for transfers between devices, body(): lax.all_to_all(outgoing, 'row', split_axis=0, concat_axis=0, tiled=True)  49 us
    all_gather x1, waiting for transfers between devices, body(): coeff_piece = lax.all_gather(coeffs, 'col', axis=1, tiled=True)  30.4 us
    dot_general x1, matrix products, product(): lax.dot_general(coeff_piece, kept_rows, (((0,), (0,)), ((), ())), preferr...  16.8 us
    unnamed x3, local copies, waits for them, and re-layouts  12 us
    all_to_all x1, starting transfers between devices, body(): lax.all_to_all(outgoing, 'row', split_axis=0, concat_axis=0, tiled=True)  7.68 us
    reshape x1, local copies, waits for them, and re-layouts, body(): incoming.reshape(slot_count, atom_w * row_width)  7.23 us
    dot_general x1, local copies, waits for them, and re-layouts, body(): jnp.dot(placing, integrals.reshape(per_dev, atom_w * row_width), preferre...  6.28 us
  transfers between devices with their start and end apart: 3, of which 3 were waited for; matrix products, arithmetic and copies ran while one was open for 12% of the time, Pallas kernels for 0%

commit v1 on v0

--- a/solution.py
+++ b/solution.py
@@ -52,7 +52,9 @@
     blocks = ordered * keep_rows[:, :, None].astype(jnp.bfloat16)
     bucket_edges = [0, per_dev]
     kept_rows = blocks.reshape(per_dev * atom_w, row_width)
-    coeff_piece = lax.all_gather(coeffs, "col", axis=1, tiled=True)
+    coeff_piece = jnp.concatenate(
+        lax.all_to_all(jnp.stack([coeffs] * lax.axis_size("col")), "col", 0, 0), axis=1
+    )
     low_row = bucket_edges[0] * atom_w
     high_row = bucket_edges[1] * atom_w
 

time: 261 us -> 458 us (1.75)
  waiting for transfers between devices: 179 us -> 361 us
  starting transfers between devices: 7.9 us -> 16.6 us
  local copies, waits for them, and re-layouts: 34.7 us -> 39.8 us
    all_to_all x0 -> x1, waiting for transfers between devices: none -> 215 us  [body(): lax.all_to_all(jnp.stack([coeffs] * lax.axis_size('col')), 'col', 0, 0)]
    all_gather x1 -> x0, waiting for transfers between devices: 30.4 us -> none  [body(): coeff_piece = lax.all_gather(coeffs, 'col', axis=1, tiled=True)]
    all_to_all x0 -> x1, starting transfers between devices: none -> 8.6 us  [body(): lax.all_to_all(jnp.stack([coeffs] * lax.axis_size('col')), 'col', 0, 0)]
    unnamed x3 -> x6, local copies, waits for them, and re-layouts: 12 us -> 12.6 us
  transfers between devices with their start and end apart: 3 -> 3, of which waited for: 3 -> 3; matrix products, arithmetic and copies ran while one was open for 12% -> 4% of each run, Pallas kernels for 0% -> 0%
where the time goes in v1:
time: 458 us; the launch traced here: 457 us
  waiting for transfers between devices  361 us (79%)
  local copies, waits for them, and re-layouts  39.8 us (9%)
  matrix products  23.6 us (5%)
  starting transfers between devices  16.6 us (4%)
  between operations  13.5 us (3%)
    all_to_all x1, waiting for transfers between devices, body(): lax.all_to_all(jnp.stack([coeffs] * lax.axis_size('col')), 'col', 0, 0)  215 us
    reduce_scatter x1, waiting for transfers between devices, body(): lax.psum_scatter(partial_sums, 'row', scatter_dimension=0, tiled=True)  95.1 us
    all_to_all x1, waiting for transfers between devices, body(): lax.all_to_all(outgoing, 'row', split_axis=0, concat_axis=0, tiled=True)  50.8 us
    dot_general x1, matrix products, product(): lax.dot_general(coeff_piece, kept_rows, (((0,), (0,)), ((), ())), preferr...  16.7 us
    unnamed x6, local copies, waits for them, and re-layouts  12.6 us
  transfers between devices with their start and end apart: 3, of which 3 were waited for; matrix products, arithmetic and copies ran while one was open for 4% of the time, Pallas kernels for 0%

profile of v1, /device:TPU:2, one launch (start us, length us, event | category | flops | bytes accessed | tf_op | source)
XLA Modules:
  0.0 457.3 jit_solution(12801380798418694993)
XLA Ops:
  6.5 0.8 and_select_fusion
  7.3 0.2 convert_reduce_fusion
  7.5 0.8 multiply_add_fusion.1
  8.3 5.3 %reshape.131 = bf16[40,32768,1]{1,0,2:T(8,128)(2,1)} reshape(bf16[40,32,1024]{2,1,0:T(8,128)(2,1)} %param.5) | data formatting | bytes 5242880 | tf_op jit(solution)/shard_map/reshape | solution.py:24
  13.5 3.0 fusion.17
  16.6 6.2 %copy.17 = bf16[32,2,32768]{2,1,0:T(2,128)(2,1)} copy(bf16[32,2,32768]{2,0,1:T(8,128)(2,1)S(1)} %fusion.17) | data formatting | bytes 8388608 | tf_op jit(solution)/shard_map/dot_general | solution.py:23
  22.8 7.8 %all-to-all-start = ((bf16[32,2,32768]{2,1,0:T(2,128)(2,1)}), bf16[32,2,32768]{2,1,0:T(2,128)(2,1)}, u32[]{:S(2)}, u32[]{:S(2)}) async-start(bf16[32,2,32768]{2,1,0:T(2,128)(2,1)} %copy.17), calls=%async_computation | async-start | bytes 8388608 | tf_op jit(solution)/shard_map/all_to_all | solution.py:27
  30.7 0.6 copy.20
  31.3 50.8 %all-to-all-done = bf16[32,2,32768]{2,1,0:T(2,128)(2,1)} async-done(((bf16[32,2,32768]{2,1,0:T(2,128)(2,1)}), bf16[32,2,32768]{2,1,0:T(2,128)(2,1)}, u32[]{:S(2)}, u32[]{:S(2)}) %all-to-all-start) | async-done | bytes 4194336 | tf_op jit(solution)/shard_map/all_to_all | solution.py:27
  82.1 4.5 stack.2
  86.6 8.6 %all-to-all-start.1 = ((bf16[8,1280,512]{1,2,0:T(8,128)(2,1)}), bf16[8,1280,512]{1,2,0:T(8,128)(2,1)}, u32[]{:S(2)}, u32[]{:S(2)}) async-start(bf16[8,1280,512]{1,2,0:T(8,128)(2,1)} %stack.2), calls=%async_computation.1 | async-start | bytes 20971520 | tf_op jit(solution)/shard_map/all_to_all | solution.py:56
  95.2 0.2 reduce-scatter.4.cloned.1.call-start
  95.4 0.1 and.41
  95.6 0.2 reduce_window_sum.11
  95.9 0.1 add.46
  96.0 0.8 dynamic_slice.10
  96.8 0.8 compare_bitcast_fusion
  97.6 7.2 %reshape.127 = bf16[64,32768]{1,0:T(8,128)(2,1)} reshape(bf16[32,2,32768]{2,1,0:T(2,128)(2,1)} %all-to-all-done) | data formatting | bytes 8388608 | tf_op jit(solution)/shard_map/reshape | solution.py:42
  104.9 3.9 fusion.3
  108.8 3.0 copy.19
  111.7 215.0 %all-to-all-done.1 = bf16[8,1280,512]{1,2,0:T(8,128)(2,1)} async-done(((bf16[8,1280,512]{1,2,0:T(8,128)(2,1)}), bf16[8,1280,512]{1,2,0:T(8,128)(2,1)}, u32[]{:S(2)}, u32[]{:S(2)}) %all-to-all-start.1) | async-done | bytes 10485792 | tf_op jit(solution)/shard_map/all_to_all | solution.py:56
  326.8 16.7 %convert_bitcast_fusion = bf16[4096,1024]{0,1:T(8,128)(2,1)} fusion(bf16[1280,1024]{1,0:T(8,128)(2,1)} %bitcast.24, bf16[1280,4096]{0,1:T(8,128)(2,1)} %bitcast.5), kind=kOutput, calls=%fused_computation | convolution fusion | flops 10741612544 | bytes 21495808 | tf_op jit(solution)/shard_map/dot_general | solution.py:62
  343.4 12.0 %copy.22 = bf16[4096,1024]{1,0:T(8,128)(2,1)} copy(bf16[4096,1024]{0,1:T(8,128)(2,1)} %convert_bitcast_fusion) | data formatting | bytes 16777216
  355.4 95.1 %reduce-scatter.4.cloned.1.call-done = bf16[128,1024]{1,0:T(8,128)(2,1)} async-done(((bf16[4096,1024]{1,0:T(8,128)(2,1)}), bf16[128,1024]{1,0:T(8,128)(2,1)}) %reduce-scatter.4.cloned.1.call-update) | async-done | bytes 262160 | tf_op jit(solution)/shard_map/reduce_scatter | solution.py:68
  (14 shorter events, 0.3 us)
Async XLA Ops:
  22.8 7.8 %copy-start = (bf16[1280,512]{1,0:T(8,128)(2,1)S(1)}, bf16[1280,512]{1,0:T(8,128)(2,1)}, u32[]{:S(2)}) copy-start(bf16[1280,512]{1,0:T(8,128)(2,1)} %param.6) | copy-start | bytes 3932164
  22.8 59.2 %all-to-all-start = ((bf16[32,2,32768]{2,1,0:T(2,128)(2,1)}), bf16[32,2,32768]{2,1,0:T(2,128)(2,1)}, u32[]{:S(2)}, u32[]{:S(2)}) async-start(bf16[32,2,32768]{2,1,0:T(2,128)(2,1)} %copy.17), calls=%async_computation | async-start | bytes 8388608 | tf_op jit(solution)/shard_map/all_to_all | solution.py:27
  86.6 8.8 %copy-start.1 = (s32[1280]{0:T(1024)S(1)}, s32[1280]{0:T(1024)}, u32[]{:S(2)}) copy-start(s32[1280]{0:T(1024)} %param.9) | copy-start | bytes 15364
  86.6 240.2 %all-to-all-start.1 = ((bf16[8,1280,512]{1,2,0:T(8,128)(2,1)}), bf16[8,1280,512]{1,2,0:T(8,128)(2,1)}, u32[]{:S(2)}, u32[]{:S(2)}) async-start(bf16[8,1280,512]{1,2,0:T(8,128)(2,1)} %stack.2), calls=%async_computation.1 | async-start | bytes 20971520 | tf_op jit(solution)/shard_map/all_to_all | solution.py:56
  95.2 355.3 %reduce-scatter.4.cloned.1.call-start = ((), (), s32[]{:S(2)}) async-start(), calls=%async_computation.3 | async-start | bytes 8650752 | tf_op jit(solution)/shard_map/reduce_scatter | solution.py:68
Sparse Core Ops, SparseCore 0:
  355.6 94.8 reduce-scatter.3
